TPU v7x, 256 devices: a whole 4x4x8 slice. The times are simulated.
256 devices in a mesh: ctx: 8 (over z), vocab: 32 (over y, x, core).
Axes of the slice: x: 4, y: 4, z: 8, core: 2. Of those that a mesh axis runs over, the one named last changes fastest.
Arguments:
- hidden: bfloat16 [16, 128, 4096], P(None, 'ctx', 'vocab'), may hold values from -6 to 6
- head_weight: bfloat16 [4096, 128256], P(None, ('ctx', 'vocab')), may hold values from -0.09375 to 0.09375
- token_ids: int32 [16, 128], P(None, 'ctx'), may hold values from 0 to 128255
- response_mask: int32 [16, 128], P(None, 'ctx'), may hold values 0 or 1
- pair_order: int32 [16], replicated, may hold values from 0 to 15, each once
- frozen_logprob: float32 [16], replicated, may hold values from -40 to 40
Outputs:
- pair_loss: float32 [], replicated
- margins: float32 [8], replicated
- head_grad: bfloat16 [4096, 128256], P(None, ('ctx', 'vocab'))
- spread_grad: bfloat16 [4096, 128256], P(None, ('ctx', 'vocab'))
Inputs may be any that keep to these rules, and one draw needn't show every extreme that they name: `token_ids`: token ids lie in 0 to 128255. `response_mask`: mask entries are 0 or 1. pair_order names every sequence exactly once; entry p is the chosen sequence of pair p and entry 8 + p the rejected one.
All inputs are finite; a program needn't handle non-finite values.
Results may differ from a plain program's by a relative error of at most 0.0015.
Values may be sent and summed in bfloat16 or wider, within the bound.
A program may use at most 128 MiB of HBM per device.

v0:
```python
import jax
import jax.numpy as jnp
from jax import lax
from jax.sharding import Mesh
from jax.sharding import PartitionSpec as P

V = 128256
VOCAB = ("vocab_0", "vocab_1", "vocab_2")
CTX_VOCAB = ("ctx", "vocab_0", "vocab_1", "vocab_2")
strength = 0.1
loss_scale = 256.0


def laid_out(pieces, dim):
    pieces = jnp.moveaxis(pieces, 0, dim)
    lengths = pieces.shape
    return pieces.reshape(*lengths[:dim], lengths[dim] * lengths[dim + 1], *lengths[dim + 2 :])


def gather_packed(arrays, axis, dims):
    flat = jnp.concatenate([a.reshape(-1) for a in arrays])
    lines, at, finished = (lax.all_gather(flat, axis), 0, [])
    for a, dim in zip(arrays, dims):
        pieces = lines[:, at : at + a.size].reshape(-1, *a.shape)
        finished.append(laid_out(pieces, dim))
        at += a.size
    return tuple(finished)


def by_axis(shard, axes):
    for axis in axes:
        shard = lax.pmax(shard, axis)
    return shard


def by_axis_2(shard, axes):
    for axis in axes:
        shard = lax.psum(shard, axis)
    return shard


def contract_rows(block_rows, both_logits):
    return lax.dot_general(
        block_rows, both_logits, (((0,), (0,)), ((), ())), preferred_element_type=jnp.float32
    )


def shards(hidden, head_weight, token_ids, response_mask, pair_order, frozen_logprob):
    seq_rows = lax.all_gather(hidden, "ctx", axis=1, tiled=True)
    ids_all, mask_all = gather_packed((token_ids, response_mask), "ctx", (1, 1))
    token_rows = seq_rows.reshape(seq_rows.shape[0] * seq_rows.shape[1], seq_rows.shape[2])
    shard_width = head_weight.shape[1]
    whole_rows = lax.all_gather(token_rows, VOCAB, axis=1, tiled=True)
    logits = jnp.dot(whole_rows, head_weight, preferred_element_type=jnp.float32)
    offset = lax.axis_index(CTX_VOCAB) * shard_width
    local_ids = ids_all.reshape(-1) - offset
    columns = jnp.arange(shard_width).astype(jnp.int32)
    onehot = (columns[None, :] == local_ids[:, None]).astype(jnp.float32)
    picked_part = jnp.sum(onehot * logits, axis=1)
    peak_part = jnp.max(logits, axis=1)
    row_peak = by_axis(peak_part, CTX_VOCAB)
    exp_sums = jnp.sum(jnp.exp(logits - row_peak[:, None]), axis=1)
    sum_total, picked = (by_axis_2(exp_sums, CTX_VOCAB), by_axis_2(picked_part, CTX_VOCAB))
    log_norm = row_peak + jnp.log(sum_total)
    mask_flat = mask_all.reshape(-1).astype(jnp.float32)
    seq_count = ids_all.shape[0]
    policy = jnp.sum(((picked - log_norm) * mask_flat).reshape(seq_count, ids_all.shape[1]), axis=1)
    log_ratio = policy - frozen_logprob
    pair_count = pair_order.shape[0] // 2
    chosen = pair_order[:pair_count]
    rejected = pair_order[pair_count:]
    margins = strength * (log_ratio[chosen] - log_ratio[rejected])
    pair_loss = jnp.mean(jax.nn.softplus(-margins))
    weight = -loss_scale * strength * jax.nn.sigmoid(-margins) / pair_count
    seq_coef = jnp.zeros((seq_count,), jnp.float32).at[chosen].set(weight).at[rejected].set(-weight)
    token_coef = (seq_coef[:, None] * mask_all.astype(jnp.float32)).reshape(-1)
    probabilities = jnp.exp(logits - log_norm[:, None])
    grad_logits = (token_coef[:, None] * (onehot - probabilities)).astype(jnp.bfloat16)
    spread_logits = (V / 64.0 * token_coef[:, None] * probabilities).astype(jnp.bfloat16)
    both_logits = jnp.concatenate([grad_logits, spread_logits], axis=1)
    both_grads = contract_rows(whole_rows, both_logits)
    head_grad = both_grads[:, :shard_width].astype(jnp.bfloat16)
    spread_grad = both_grads[:, shard_width:].astype(jnp.bfloat16)
    return (pair_loss, margins, head_grad, spread_grad)


def solution(mesh):
    split = Mesh(
        mesh.devices.reshape(mesh.shape["ctx"], 4, 4, 2), ("ctx", "vocab_0", "vocab_1", "vocab_2")
    )
    placed = (P(None, "ctx", VOCAB), P(None, CTX_VOCAB), P(None, "ctx"), P(None, "ctx"), P(), P())
    return jax.shard_map(
        shards,
        mesh=split,
        in_specs=placed,
        out_specs=(P(), P(), P(None, CTX_VOCAB), P(None, CTX_VOCAB)),
        check_vma=False,
    )
```

profile of v0, /device:TPU:1, one launch (start us, length us, event | category | flops | bytes accessed | tf_op | source)
XLA Modules:
  0.0 282.0 jit_solution(17380326910799111413)
XLA Ops:
  7.2 26.5 %all_gather.14 = bf16[16,128,128]{2,1,0:T(8,128)(2,1)} all-gather(bf16[16,16,128]{2,1,0:T(8,128)(2,1)} %param.6), channel_id=1, replica_groups=mesh['ctx'=8,'vocab_0'=4,'vocab_1'=4,'vocab_2'=2] {'ctx'}, dimensions={1}, use_global_device_ids=true | all-gather | bytes 589824 | tf_op jit(solution)/shard_map/all_gather | solution.py:49
  33.7 0.8 reshape.60
  34.5 0.8 reshape.61
  35.3 16.1 %all-gather.1 = s32[8,1,512]{2,1,0:T(1,128)S(1)} all-gather(s32[1,1,512]{2,1,0:T(1,128)S(1)} %bitcast.21), channel_id=2, replica_groups=mesh['ctx'=8,'vocab_0'=4,'vocab_1'=4,'vocab_2'=2] {'ctx'}, dimensions={0}, use_global_device_ids=true | all-gather | bytes 18432 | tf_op jit(solution)/shard_map/all_gather | solution.py:22
  51.8 0.8 compare_select_fusion.1
  52.6 71.6 %all-gather.4.cloned.1.call-done = bf16[2048,4096]{1,0:T(8,128)(2,1)} async-done(((bf16[2048,128]{1,0:T(8,128)(2,1)}), bf16[2048,4096]{1,0:T(8,128)(2,1)}) %all-gather.4.cloned.1.call-update) | async-done | bytes 16777232 | tf_op jit(solution)/shard_map/all_gather | solution.py:53
  124.2 14.8 %fusion.9 = (f32[2048]{0:T(1024)S(1)}, f32[2048,501]{0,1:T(8,128)}) fusion(bf16[2048,4096]{1,0:T(8,128)(2,1)} %all-gather.4.cloned.1.call-done, bf16[4096,501]{0,1:T(8,128)(2,1)} %param.7), kind=kOutput, calls=%fused_computation.35 | convolution fusion | flops 8406409216 | bytes 24993792 | tf_op jit(solution)/shard_map/dot_general | solution.py:54
  139.0 14.1 %pmax.28 = f32[2048]{0:T(1024)S(1)} all-reduce(f32[2048]{0:T(1024)S(1)} %get-tuple-element.29), channel_id=1, replica_groups=mesh['ctx'=8,'vocab_0'=4,'vocab_1'=4,'vocab_2'=2] {'ctx'}, use_global_device_ids=true, to_apply=%region_6.0 | all-reduce | flops 2048 | bytes 16384 | tf_op jit(solution)/shard_map/pmax | solution.py:32
  153.1 8.2 %pmax.29 = f32[2048]{0:T(1024)S(1)} all-reduce(f32[2048]{0:T(1024)S(1)} %pmax.28), channel_id=1, replica_groups=mesh['ctx'=8,'vocab_0'=4,'vocab_1'=4,'vocab_2'=2] {'vocab_0'}, use_global_device_ids=true, to_apply=%region_7.0 | all-reduce | flops 2048 | bytes 16384 | tf_op jit(solution)/shard_map/pmax | solution.py:32
  161.3 7.4 %pmax.30 = f32[2048]{0:T(1024)S(1)} all-reduce(f32[2048]{0:T(1024)S(1)} %pmax.29), channel_id=1, replica_groups=mesh['ctx'=8,'vocab_0'=4,'vocab_1'=4,'vocab_2'=2] {'vocab_1'}, use_global_device_ids=true, to_apply=%region_8.0 | all-reduce | flops 2048 | bytes 16384 | tf_op jit(solution)/shard_map/pmax | solution.py:32
  168.7 10.1 %pmax.31 = f32[2048]{0:T(1024)S(1)} all-reduce(f32[2048]{0:T(1024)S(1)} %pmax.30), channel_id=1, replica_groups=mesh['ctx'=8,'vocab_0'=4,'vocab_1'=4,'vocab_2'=2] {'vocab_2'}, use_global_device_ids=true, to_apply=%region_9.0 | all-reduce | flops 2048 | bytes 16384 | tf_op jit(solution)/shard_map/pmax | solution.py:32
  178.8 3.3 %exponential_reduce_fusion = (f32[2048]{0:T(1024)S(1)}, f32[2048]{0:T(1024)S(1)}) fusion(f32[2048,501]{0,1:T(8,128)} %get-tuple-element.30, f32[2048]{0:T(1024)S(1)} %pmax.31, s32[2048]{0:T(1024)S(1)} %sub.51), kind=kLoop, calls=%fused_computation.11 | loop fusion | flops 5126144 | bytes 4136960 | tf_op jit(solution)/shard_map/reduce_sum | solution.py:62
  182.1 20.5 %all-reduce = (f32[2048]{0:T(1024)S(1)}, f32[2048]{0:T(1024)S(1)}) all-reduce(f32[2048]{0:T(1024)S(1)} %get-tuple-element.5, f32[2048]{0:T(1024)S(1)} %get-tuple-element.4), channel_id=1, replica_groups=mesh['ctx'=8,'vocab_0'=4,'vocab_1'=4,'vocab_2'=2] {'ctx'}, use_global_device_ids=true, to_apply=%region_1.0 | all-reduce | flops 4096 | bytes 32768 | tf_op jit(solution)/shard_map/psum | solution.py:38
  202.6 10.8 %all-reduce.2 = (f32[2048]{0:T(1024)S(1)}, f32[2048]{0:T(1024)S(1)}) all-reduce(f32[2048]{0:T(1024)S(1)} %get-tuple-element.6, f32[2048]{0:T(1024)S(1)} %get-tuple-element.7), channel_id=1, replica_groups=mesh['ctx'=8,'vocab_0'=4,'vocab_1'=4,'vocab_2'=2] {'vocab_0'}, use_global_device_ids=true, to_apply=%region_2.0 | all-reduce | flops 4096 | bytes 32768 | tf_op jit(solution)/shard_map/psum | solution.py:38
  213.4 10.9 %all-reduce.1 = (f32[2048]{0:T(1024)S(1)}, f32[2048]{0:T(1024)S(1)}) all-reduce(f32[2048]{0:T(1024)S(1)} %get-tuple-element.10, f32[2048]{0:T(1024)S(1)} %get-tuple-element.11), channel_id=1, replica_groups=mesh['ctx'=8,'vocab_0'=4,'vocab_1'=4,'vocab_2'=2] {'vocab_1'}, use_global_device_ids=true, to_apply=%region_3.0 | all-reduce | flops 4096 | bytes 32768 | tf_op jit(solution)/shard_map/psum | solution.py:38
  224.3 17.9 %all-reduce.3 = (f32[2048]{0:T(1024)S(1)}, f32[2048]{0:T(1024)S(1)}) all-reduce(f32[2048]{0:T(1024)S(1)} %get-tuple-element.8, f32[2048]{0:T(1024)S(1)} %get-tuple-element.9), channel_id=1, replica_groups=mesh['ctx'=8,'vocab_0'=4,'vocab_1'=4,'vocab_2'=2] {'vocab_2'}, use_global_device_ids=true, to_apply=%region_4.0 | all-reduce | flops 4096 | bytes 32768 | tf_op jit(solution)/shard_map/psum | solution.py:38
  242.3 0.6 gather_fusion.1
  243.0 0.6 gather_fusion
  243.7 0.6 scatter_custom_fusion
  244.3 0.8 scatter_fusion
  245.1 3.5 %multiply_convert_fusion.1 = (bf16[2048,501]{0,1:T(8,128)(2,1)S(1)}, bf16[2048,501]{0,1:T(8,128)(2,1)S(1)}) fusion(f32[2048,501]{0,1:T(8,128)} %get-tuple-element.30, f32[2048]{0:T(1024)S(1)} %get-tuple-element.20, f32[2048]{0:T(1024)S(1)} %get-tuple-element.15, s32[2048]{0:T(1024)S(1)} %sub.51, f32[2048]{0:T(1024)S(1)} %get-tuple-element.14), kind=kLoop, calls=%fused_computation.9 | loop fusion | flops 8208384 | bytes 8241152 | tf_op jit(solution)/shard_map/convert_element_type | solution.py:78
  248.7 20.1 %convert_bitcast_fusion = bf16[4096,1002]{0,1:T(8,128)(2,1)S(1)} fusion(bf16[2048,4096]{1,0:T(8,128)(2,1)} %all-gather.4.cloned.1.call-done, bf16[2048,501]{0,1:T(8,128)(2,1)S(1)} %get-tuple-element.24, bf16[2048,501]{0,1:T(8,128)(2,1)S(1)} %get-tuple-element.23), kind=kOutput, calls=%fused_computation.4 | convolution fusion | flops 16823083008 | bytes 29089792 | tf_op jit(solution)/shard_map/dot_general | solution.py:43
  268.7 4.0 %fusion.8 = (bf16[4096,501]{0,1:T(8,128)(2,1)}, bf16[4096,501]{0,1:T(8,128)(2,1)}) fusion(bf16[4096,1002]{0,1:T(8,128)(2,1)S(1)} %convert_bitcast_fusion), kind=kLoop, calls=%fused_computation.34 | loop fusion | bytes 16416768 | tf_op jit(solution)/shard_map/slice | solution.py:83
  272.7 0.6 fusion.3
  (20 shorter events, 0.7 us)
Async XLA Ops:
  7.2 117.1 %all-gather.4.cloned.1.call-start = ((), (), s32[]{:S(2)}) async-start(), calls=%async_computation | async-start | bytes 17301504 | tf_op jit(solution)/shard_map/all_gather | solution.py:53
  139.0 103.3 %copy-start.1 = (f32[16]{0:T(128)S(1)}, f32[16]{0:T(128)}, u32[]{:S(2)}) copy-start(f32[16]{0:T(128)} %param.11) | copy-start | bytes 196
  243.6 29.1 %copy-start = (f32[8]{0:T(128)}, f32[8]{0:T(128)S(1)}, u32[]{:S(2)}) copy-start(f32[8]{0:T(128)S(1)} %get-tuple-element.18) | copy-start | bytes 100
Sparse Core Ops, SparseCore 0:
  33.8 90.3 all-gather.3
where the time goes:
time: 282 us
  blocking collectives  142 us (50%)
  waiting for transfers between devices  71.7 us (25%)
  matrix products  34.9 us (12%)
  between operations  15.9 us (6%)
  local copies, waits for them, and re-layouts  8.61 us (3%)
  other arithmetic  8.44 us (3%)
    all_gather x1, waiting for transfers between devices, shards(): whole_rows = lax.all_gather(token_rows, VOCAB, axis=1, tiled=True)  71.6 us
    psum x4, blocking collectives, by_axis_2(): shard = lax.psum(shard, axis)  60.1 us
    pmax x4, blocking collectives, by_axis(): shard = lax.pmax(shard, axis)  39.7 us
    all_gather x1, blocking collectives, shards(): seq_rows = lax.all_gather(hidden, 'ctx', axis=1, tiled=True)  26.5 us
    dot_general x1, matrix products, contract_rows(): lax.dot_general(block_rows, both_logits, (((0,), (0,)), ((), ())), prefer...  20.1 us
    all_gather x1, blocking collectives, gather_packed(): lines, at, finished = (lax.all_gather(flat, axis), 0, [])  16.1 us
    dot_general x1, matrix products, shards(): jnp.dot(whole_rows, head_weight, preferred_element_type=jnp.float32)  14.8 us
  transfers between devices with their start and end apart: 1, of which 1 were waited for; matrix products, arithmetic and copies ran while one was open for 1% of the time, Pallas kernels for 0%

commit v1 on v0

--- a/solution.py
+++ b/solution.py
@@ -46,7 +46,17 @@
 
 
 def shards(hidden, head_weight, token_ids, response_mask, pair_order, frozen_logprob):
-    seq_rows = lax.all_gather(hidden, "ctx", axis=1, tiled=True)
+    amount_of = lax.psum(1, "ctx")
+    column = [(i0, (i0 + 1) % amount_of) for i0 in range(amount_of)]
+    frames = [(i0, (i0 - 1) % amount_of) for i0 in range(amount_of)]
+    s_next, out_arr = ([hidden], [hidden])
+    for _ in range(amount_of // 2):
+        s_next.append(lax.ppermute(s_next[-1], "ctx", column))
+    for _ in range((amount_of - 1) // 2):
+        local_next = lax.ppermute(out_arr[-1], "ctx", frames)
+        out_arr.append(local_next)
+    q_next = jnp.concatenate([*s_next[::-1], *out_arr[1:]], axis=1)
+    seq_rows = jnp.roll(q_next, (lax.axis_index("ctx") - amount_of // 2) * hidden.shape[1], axis=1)
     ids_all, mask_all = gather_packed((token_ids, response_mask), "ctx", (1, 1))
     token_rows = seq_rows.reshape(seq_rows.shape[0] * seq_rows.shape[1], seq_rows.shape[2])
     shard_width = head_weight.shape[1]

time: 282 us -> 280 us (level)
  blocking collectives: 142 us -> 117 us
  starting transfers between devices: 0.04 us -> 11 us
  waiting for transfers between devices: 71.7 us -> 81.6 us
    all_gather x1 -> x0, blocking collectives: 26.5 us -> none  [shards(): seq_rows = lax.all_gather(hidden, 'ctx', axis=1, tiled=True)]
    ppermute x0 -> x7, starting transfers between devices: none -> 11 us  [the longest x3 8.44 us: shards(): local_next = lax.ppermute(out_arr[-1], 'ctx', frames)]
    ppermute x0 -> x7, waiting for transfers between devices: none -> 10.3 us  [the longest x4 10.3 us: shards(): s_next.append(lax.ppermute(s_next[-1], 'ctx', column))]
  transfers between devices with their start and end apart: 1 -> 8, of which waited for: 1 -> 5; matrix products, arithmetic and copies ran while one was open for 1% -> 1% of each run, Pallas kernels for 0% -> 0%
where the time goes in v1:
time: 280 us; the launch traced here: 279 us
  blocking collectives  117 us (42%)
  waiting for transfers between devices  81.6 us (29%)
  matrix products  34.8 us (12%)
  between operations  16 us (6%)
  local copies, waits for them, and re-layouts  11.3 us (4%)
  starting transfers between devices  11 us (4%)
  other arithmetic  7.72 us (3%)
    all_gather x1, waiting for transfers between devices, shards(): whole_rows = lax.all_gather(token_rows, VOCAB, axis=1, tiled=True)  71.2 us
    psum x4, blocking collectives, by_axis_2(): shard = lax.psum(shard, axis)  60.1 us
    pmax x4, blocking collectives, by_axis(): shard = lax.pmax(shard, axis)  39.8 us
    dot_general x1, matrix products, contract_rows(): lax.dot_general(block_rows, both_logits, (((0,), (0,)), ((), ())), prefer...  20 us
    all_gather x1, blocking collectives, gather_packed(): lines, at, finished = (lax.all_gather(flat, axis), 0, [])  16.9 us
    dot_general x1, matrix products, shards(): jnp.dot(whole_rows, head_weight, preferred_element_type=jnp.float32)  14.8 us
    ppermute x4, waiting for transfers between devices, shards(): s_next.append(lax.ppermute(s_next[-1], 'ctx', column))  10.3 us
    ppermute x3, starting transfers between devices, shards(): local_next = lax.ppermute(out_arr[-1], 'ctx', frames)  8.44 us
  transfers between devices with their start and end apart: 8, of which 5 were waited for; matrix products, arithmetic and copies ran while one was open for 1% of the time, Pallas kernels for 0%

profile of v1, /device:TPU:1, one launch (start us, length us, event | category | flops | bytes accessed | tf_op | source)
XLA Modules:
  0.0 279.2 jit_solution(6724973408437147798)
XLA Ops:
  7.2 2.5 collective-permute-start
  9.8 5.8 %collective-permute-done = bf16[16,16,128]{2,1,0:T(8,128)(2,1)S(1)} collective-permute-done((bf16[16,16,128]{2,1,0:T(8,128)(2,1)}, bf16[16,16,128]{2,1,0:T(8,128)(2,1)S(1)}, u32[]{:S(2)}, u32[]{:S(2)}) %collective-permute-start) | collective-permute-done | bytes 65568 | tf_op jit(solution)/shard_map/ppermute | solution.py:54
  15.6 2.7 collective-permute-start.4
  18.2 1.6 collective-permute-done.1
  19.9 2.9 %collective-permute-start.5 = (bf16[16,16,128]{2,1,0:T(8,128)(2,1)S(1)}, bf16[16,16,128]{2,1,0:T(8,128)(2,1)S(1)}, u32[]{:S(2)}, u32[]{:S(2)}) collective-permute-start(bf16[16,16,128]{2,1,0:T(8,128)(2,1)S(1)} %collective-permute-done.4), channel_id=1, source_target_pairs={{0,224},{32,0},{64,32},{96,64},{128,96},{160,128},{192,160},{224,1... | collective-permute-start | bytes 196616 | tf_op jit(solution)/shard_map/ppermute | solution.py:56
  22.8 1.4 collective-permute-done.2
  24.2 2.9 %collective-permute-start.6 = (bf16[16,16,128]{2,1,0:T(8,128)(2,1)S(1)}, bf16[16,16,128]{2,1,0:T(8,128)(2,1)S(1)}, u32[]{:S(2)}, u32[]{:S(2)}) collective-permute-start(bf16[16,16,128]{2,1,0:T(8,128)(2,1)S(1)} %collective-permute-done.5), channel_id=1, source_target_pairs={{0,224},{32,0},{64,32},{96,64},{128,96},{160,128},{192,160},{224,1... | collective-permute-start | bytes 196616 | tf_op jit(solution)/shard_map/ppermute | solution.py:56
  27.1 1.4 collective-permute-done.3
  29.6 0.9 constant_dynamic-update-slice_fusion.3
  33.0 16.9 %all-gather.1 = s32[8,1,512]{2,1,0:T(1,128)S(1)} all-gather(s32[1,1,512]{2,1,0:T(1,128)S(1)} %bitcast.19), channel_id=2, replica_groups=mesh['ctx'=8,'vocab_0'=4,'vocab_1'=4,'vocab_2'=2] {'ctx'}, dimensions={0}, use_global_device_ids=true | all-gather | bytes 18432 | tf_op jit(solution)/shard_map/all_gather | solution.py:22
  50.3 71.2 %all-gather.4.cloned.1.call-done = bf16[2048,4096]{1,0:T(8,128)(2,1)} async-done(((bf16[2048,128]{1,0:T(8,128)(2,1)}), bf16[2048,4096]{1,0:T(8,128)(2,1)}) %all-gather.4.cloned.1.call-update) | async-done | bytes 16777232 | tf_op jit(solution)/shard_map/all_gather | solution.py:63
  121.5 14.8 %fusion.9 = (f32[2048]{0:T(1024)S(1)}, f32[2048,501]{0,1:T(8,128)}) fusion(bf16[2048,4096]{1,0:T(8,128)(2,1)} %all-gather.4.cloned.1.call-done, bf16[4096,501]{0,1:T(8,128)(2,1)} %param.7), kind=kOutput, calls=%fused_computation.52 | convolution fusion | flops 8406409216 | bytes 24993792 | tf_op jit(solution)/shard_map/dot_general | solution.py:64
  136.3 14.1 %pmax.28 = f32[2048]{0:T(1024)S(1)} all-reduce(f32[2048]{0:T(1024)S(1)} %get-tuple-element.29), channel_id=1, replica_groups=mesh['ctx'=8,'vocab_0'=4,'vocab_1'=4,'vocab_2'=2] {'ctx'}, use_global_device_ids=true, to_apply=%region_6.7 | all-reduce | flops 2048 | bytes 16384 | tf_op jit(solution)/shard_map/pmax | solution.py:32
  150.4 8.2 %pmax.29 = f32[2048]{0:T(1024)S(1)} all-reduce(f32[2048]{0:T(1024)S(1)} %pmax.28), channel_id=1, replica_groups=mesh['ctx'=8,'vocab_0'=4,'vocab_1'=4,'vocab_2'=2] {'vocab_0'}, use_global_device_ids=true, to_apply=%region_7.8 | all-reduce | flops 2048 | bytes 16384 | tf_op jit(solution)/shard_map/pmax | solution.py:32
  158.6 7.4 %pmax.30 = f32[2048]{0:T(1024)S(1)} all-reduce(f32[2048]{0:T(1024)S(1)} %pmax.29), channel_id=1, replica_groups=mesh['ctx'=8,'vocab_0'=4,'vocab_1'=4,'vocab_2'=2] {'vocab_1'}, use_global_device_ids=true, to_apply=%region_8.9 | all-reduce | flops 2048 | bytes 16384 | tf_op jit(solution)/shard_map/pmax | solution.py:32
  166.0 10.1 %pmax.31 = f32[2048]{0:T(1024)S(1)} all-reduce(f32[2048]{0:T(1024)S(1)} %pmax.30), channel_id=1, replica_groups=mesh['ctx'=8,'vocab_0'=4,'vocab_1'=4,'vocab_2'=2] {'vocab_2'}, use_global_device_ids=true, to_apply=%region_9.10 | all-reduce | flops 2048 | bytes 16384 | tf_op jit(solution)/shard_map/pmax | solution.py:32
  176.1 3.3 %exponential_reduce_fusion = (f32[2048]{0:T(1024)S(1)}, f32[2048]{0:T(1024)S(1)}) fusion(f32[2048,501]{0,1:T(8,128)} %get-tuple-element.30, f32[2048]{0:T(1024)S(1)} %pmax.31, s32[2048]{0:T(1024)S(1)} %sub.58), kind=kLoop, calls=%fused_computation.11 | loop fusion | flops 5126144 | bytes 4136960 | tf_op jit(solution)/shard_map/reduce_sum | solution.py:72
  179.4 20.5 %all-reduce = (f32[2048]{0:T(1024)S(1)}, f32[2048]{0:T(1024)S(1)}) all-reduce(f32[2048]{0:T(1024)S(1)} %get-tuple-element.5, f32[2048]{0:T(1024)S(1)} %get-tuple-element.4), channel_id=1, replica_groups=mesh['ctx'=8,'vocab_0'=4,'vocab_1'=4,'vocab_2'=2] {'ctx'}, use_global_device_ids=true, to_apply=%region_1.2 | all-reduce | flops 4096 | bytes 32768 | tf_op jit(solution)/shard_map/psum | solution.py:38
  199.9 10.8 %all-reduce.2 = (f32[2048]{0:T(1024)S(1)}, f32[2048]{0:T(1024)S(1)}) all-reduce(f32[2048]{0:T(1024)S(1)} %get-tuple-element.6, f32[2048]{0:T(1024)S(1)} %get-tuple-element.7), channel_id=1, replica_groups=mesh['ctx'=8,'vocab_0'=4,'vocab_1'=4,'vocab_2'=2] {'vocab_0'}, use_global_device_ids=true, to_apply=%region_2.3 | all-reduce | flops 4096 | bytes 32768 | tf_op jit(solution)/shard_map/psum | solution.py:38
  210.7 10.9 %all-reduce.1 = (f32[2048]{0:T(1024)S(1)}, f32[2048]{0:T(1024)S(1)}) all-reduce(f32[2048]{0:T(1024)S(1)} %get-tuple-element.10, f32[2048]{0:T(1024)S(1)} %get-tuple-element.11), channel_id=1, replica_groups=mesh['ctx'=8,'vocab_0'=4,'vocab_1'=4,'vocab_2'=2] {'vocab_1'}, use_global_device_ids=true, to_apply=%region_3.4 | all-reduce | flops 4096 | bytes 32768 | tf_op jit(solution)/shard_map/psum | solution.py:38
  221.6 17.9 %all-reduce.3 = (f32[2048]{0:T(1024)S(1)}, f32[2048]{0:T(1024)S(1)}) all-reduce(f32[2048]{0:T(1024)S(1)} %get-tuple-element.8, f32[2048]{0:T(1024)S(1)} %get-tuple-element.9), channel_id=1, replica_groups=mesh['ctx'=8,'vocab_0'=4,'vocab_1'=4,'vocab_2'=2] {'vocab_2'}, use_global_device_ids=true, to_apply=%region_4.5 | all-reduce | flops 4096 | bytes 32768 | tf_op jit(solution)/shard_map/psum | solution.py:38
  242.2 3.5 %multiply_convert_fusion.1 = (bf16[2048,501]{0,1:T(8,128)(2,1)S(1)}, bf16[2048,501]{0,1:T(8,128)(2,1)S(1)}) fusion(f32[2048,501]{0,1:T(8,128)} %get-tuple-element.30, f32[2048]{0:T(1024)S(1)} %get-tuple-element.20, f32[2048]{0:T(1024)S(1)} %get-tuple-element.15, s32[2048]{0:T(1024)S(1)} %sub.58, f32[2048]{0:T(1024)S(1)} %get-tuple-element.14), kind=kLoop, calls=%fused_computation.9 | loop fusion | flops 8208384 | bytes 8241152 | tf_op jit(solution)/shard_map/convert_element_type | solution.py:88
  245.8 20.0 %convolution_convert_fusion = bf16[4096,1002]{0,1:T(8,128)(2,1)S(1)} fusion(bf16[2048,4096]{1,0:T(8,128)(2,1)} %all-gather.4.cloned.1.call-done, bf16[2048,501]{0,1:T(8,128)(2,1)S(1)} %get-tuple-element.24, bf16[2048,501]{0,1:T(8,128)(2,1)S(1)} %get-tuple-element.23), kind=kOutput, calls=%fused_computation.4 | convolution fusion | flops 16823083008 | bytes 29089792 | tf_op jit(solution)/shard_map/dot_general | solution.py:43
  265.8 4.1 %fusion.8 = (bf16[4096,501]{0,1:T(8,128)(2,1)}, bf16[4096,501]{0,1:T(8,128)(2,1)}) fusion(bf16[4096,1002]{0,1:T(8,128)(2,1)S(1)} %convolution_convert_fusion), kind=kLoop, calls=%fused_computation.51 | loop fusion | bytes 16416768 | tf_op jit(solution)/shard_map/slice | solution.py:93
  (52 shorter events, 7.3 us)
Async XLA Ops:
  7.2 43.1 %copy-start = (s32[16]{0:T(128)S(1)}, s32[16]{0:T(128)}, u32[]{:S(2)}) copy-start(s32[16]{0:T(128)} %param.10) | copy-start | bytes 196
  7.2 114.4 %all-gather.4.cloned.1.call-start = ((), (), s32[]{:S(2)}) async-start(), calls=%async_computation | async-start | bytes 17301504 | tf_op jit(solution)/shard_map/all_gather | solution.py:63
  7.2 8.3 %collective-permute-start = (bf16[16,16,128]{2,1,0:T(8,128)(2,1)}, bf16[16,16,128]{2,1,0:T(8,128)(2,1)S(1)}, u32[]{:S(2)}, u32[]{:S(2)}) collective-permute-start(bf16[16,16,128]{2,1,0:T(8,128)(2,1)} %param.6), channel_id=1, source_target_pairs={{0,32},{32,64},{64,96},{96,128},{128,160},{160,192},{192,224},{224... | collective-permute-start | bytes 196616 | tf_op jit(solution)/shard_map/ppermute | solution.py:54
  15.6 4.3 %collective-permute-start.1 = (bf16[16,16,128]{2,1,0:T(8,128)(2,1)S(1)}, bf16[16,16,128]{2,1,0:T(8,128)(2,1)S(1)}, u32[]{:S(2)}, u32[]{:S(2)}) collective-permute-start(bf16[16,16,128]{2,1,0:T(8,128)(2,1)S(1)} %collective-permute-done), channel_id=1, source_target_pairs={{0,32},{32,64},{64,96},{96,128},{128,160},{160,192},{192,224},{224... | collective-permute-start | bytes 196616 | tf_op jit(solution)/shard_map/ppermute | solution.py:54
  15.6 4.3 %collective-permute-start.4 = (bf16[16,16,128]{2,1,0:T(8,128)(2,1)}, bf16[16,16,128]{2,1,0:T(8,128)(2,1)S(1)}, u32[]{:S(2)}, u32[]{:S(2)}) collective-permute-start(bf16[16,16,128]{2,1,0:T(8,128)(2,1)} %param.6), channel_id=1, source_target_pairs={{0,224},{32,0},{64,32},{96,64},{128,96},{160,128},{192,160},{224,1... | collective-permute-start | bytes 196616 | tf_op jit(solution)/shard_map/ppermute | solution.py:56
  19.9 4.3 %collective-permute-start.2 = (bf16[16,16,128]{2,1,0:T(8,128)(2,1)S(1)}, bf16[16,16,128]{2,1,0:T(8,128)(2,1)S(1)}, u32[]{:S(2)}, u32[]{:S(2)}) collective-permute-start(bf16[16,16,128]{2,1,0:T(8,128)(2,1)S(1)} %collective-permute-done.1), channel_id=1, source_target_pairs={{0,32},{32,64},{64,96},{96,128},{128,160},{160,192},{192,224},{224... | collective-permute-start | bytes 196616 | tf_op jit(solution)/shard_map/ppermute | solution.py:54
  19.9 4.3 %collective-permute-start.5 = (bf16[16,16,128]{2,1,0:T(8,128)(2,1)S(1)}, bf16[16,16,128]{2,1,0:T(8,128)(2,1)S(1)}, u32[]{:S(2)}, u32[]{:S(2)}) collective-permute-start(bf16[16,16,128]{2,1,0:T(8,128)(2,1)S(1)} %collective-permute-done.4), channel_id=1, source_target_pairs={{0,224},{32,0},{64,32},{96,64},{128,96},{160,128},{192,160},{224,1... | collective-permute-start | bytes 196616 | tf_op jit(solution)/shard_map/ppermute | solution.py:56
  24.2 4.3 %collective-permute-start.3 = (bf16[16,16,128]{2,1,0:T(8,128)(2,1)S(1)}, bf16[16,16,128]{2,1,0:T(8,128)(2,1)S(1)}, u32[]{:S(2)}, u32[]{:S(2)}) collective-permute-start(bf16[16,16,128]{2,1,0:T(8,128)(2,1)S(1)} %collective-permute-done.2), channel_id=1, source_target_pairs={{0,32},{32,64},{64,96},{96,128},{128,160},{160,192},{192,224},{224... | collective-permute-start | bytes 196616 | tf_op jit(solution)/shard_map/ppermute | solution.py:54
  24.2 5.3 %collective-permute-start.6 = (bf16[16,16,128]{2,1,0:T(8,128)(2,1)S(1)}, bf16[16,16,128]{2,1,0:T(8,128)(2,1)S(1)}, u32[]{:S(2)}, u32[]{:S(2)}) collective-permute-start(bf16[16,16,128]{2,1,0:T(8,128)(2,1)S(1)} %collective-permute-done.5), channel_id=1, source_target_pairs={{0,224},{32,0},{64,32},{96,64},{128,96},{160,128},{192,160},{224,1... | collective-permute-start | bytes 196616 | tf_op jit(solution)/shard_map/ppermute | solution.py:56
  136.3 103.3 %copy-start.2 = (f32[16]{0:T(128)S(1)}, f32[16]{0:T(128)}, u32[]{:S(2)}) copy-start(f32[16]{0:T(128)} %param.11) | copy-start | bytes 196
  240.9 29.0 %copy-start.1 = (f32[8]{0:T(128)}, f32[8]{0:T(128)S(1)}, u32[]{:S(2)}) copy-start(f32[8]{0:T(128)S(1)} %get-tuple-element.18) | copy-start | bytes 100
Sparse Core Ops, SparseCore 0:
  31.5 89.9 all-gather.3
